TPU v7x, 128 devices: a whole 4x4x4 slice. The times are simulated.
128 devices in a mesh: dom: 8 (over x, core), grp: 16 (over z, y).
Axes of the slice: x: 4, y: 4, z: 4, core: 2. Of those that a mesh axis runs over, the one named last changes fastest.
Arguments:
- features: bfloat16 [524288, 256], P(('dom', 'grp')), may hold values from -6 to 6
- w_fine: bfloat16 [256, 256], replicated, may hold values from -0.375 to 0.375
- adj_tiles: bfloat16 [4096, 20, 128, 128], P(('dom', 'grp')), may hold values from -0.125 to 0.125
- tile_cols: int32 [4096, 20], P(('dom', 'grp')), may hold values from 0 to 39
- tile_count: int32 [4096], P(('dom', 'grp')), may hold values from 1 to 20, as said below
- send_lower: int32 [512], P(('dom', 'grp')), may hold values from 0 to 31
- send_upper: int32 [512], P(('dom', 'grp')), may hold values from 0 to 31
- assign: int32 [524288], P(('dom', 'grp')), may hold values from 0 to 1023, as said below
- w_coarse: bfloat16 [256, 256], replicated, may hold values from -0.375 to 0.375
- coarse_adj: bfloat16 [1024, 1024], P(('dom', 'grp')), may hold values from -0.1875 to 0.1875
Outputs:
- output: bfloat16 [524288, 256], P(('dom', 'grp'))
Inputs may be any that keep to these rules, and one draw needn't show every extreme that they name: The first tile_count[r] slots of block row r are live; the others are ignored. `assign`: every coarse node is the coarse node of at least one vertex.
All inputs are finite; a program needn't handle non-finite values.
Results may differ from a plain program's by a relative error of at most 0.011.
Values may be sent and summed in bfloat16 or wider, within the bound.
A program may use at most 192 MiB of HBM per device.

v0:
```python
import math

import jax
import jax.numpy as jnp
from jax import lax
from jax.sharding import Mesh
from jax.sharding import PartitionSpec as P

NC = 1024
DOM = ("dom_0", "dom_1")
GRP = ("grp_0", "grp_1")
DOM_GRP = ("dom_0", "dom_1", "grp_0", "grp_1")


def with_halo(shard, sides, width):
    for axis, dim in sides:
        peers, length = (lax.axis_size(axis), shard.shape[dim])
        up = [(i, (i + 1) % peers) for i in range(peers)]
        down = [(j, i) for i, j in up]
        last = lax.slice_in_dim(shard, length - width, length, axis=dim)
        initial = lax.slice_in_dim(shard, 0, width, axis=dim)
        before = lax.ppermute(last, axis, up)
        after = lax.ppermute(initial, axis, down)
        shard = jnp.concatenate([before, shard, after], axis=dim)
    return shard


def in_blocks(shard, dim, peers):
    dims = shard.shape
    blocks = shard.reshape(*dims[:dim], peers, dims[dim] // peers, *dims[dim + 1 :])
    return jnp.moveaxis(blocks, dim, 0)


def sent_and_summed(shard, axis, dim):
    peers = lax.axis_size(axis)
    blocks = lax.all_to_all(in_blocks(shard, dim, peers), axis, 0, 0, tiled=True)
    return jnp.sum(blocks.astype(jnp.float32), axis=0)


def sent_together(arrays, axis, dim, along):
    widths = [math.prod(a.shape[along:]) for a in arrays]
    both = jnp.concatenate(
        [a.reshape(*a.shape[:along], w) for a, w in zip(arrays, widths)], axis=along
    )
    whole = sent_and_summed(both, axis, dim)
    blocks = jnp.split(whole, [sum(widths[:k]) for k in range(1, len(widths))], axis=along)
    return tuple(
        (b.reshape(*whole.shape[:along], *a.shape[along:]) for a, b in zip(arrays, blocks))
    )


def from_everyone(shard, axis):
    peers = lax.axis_size(axis)
    return lax.all_to_all(
        jnp.broadcast_to(shard[None], (peers, *shard.shape)), axis, 0, 0, tiled=True
    )


def over_copies(shard, axis):
    everything = from_everyone(shard, axis)
    return jnp.sum(everything.astype(jnp.float32), axis=0)


def laid_out(blocks, dim):
    dims = list(blocks.shape[1:])
    dims[dim] *= blocks.shape[0]
    return jnp.moveaxis(blocks, 0, dim).reshape(dims)


def collect(shard, axis, dim):
    return laid_out(from_everyone(shard, axis), dim)


def gather_in_order(shard, axes, order):
    blocks = shard
    for k in order:
        blocks = lax.all_gather(blocks, axes[k])
    done = order[::-1]
    back = [done.index(k) for k in range(len(axes))]
    blocks = blocks.transpose(*back, *range(len(axes), blocks.ndim))
    return blocks.reshape(-1, *shard.shape)


def gather_axes(shard, axes, order, dim):
    return laid_out(gather_in_order(shard, axes, order), dim)


def finish(coarse_sums, counts, w_coarse):
    coarse = (coarse_sums / jnp.sqrt(counts)[:, None]).astype(jnp.bfloat16)
    return jnp.dot(coarse, w_coarse, preferred_element_type=jnp.float32).astype(jnp.bfloat16)


def per_device(
    features,
    w_fine,
    adj_tiles,
    tile_cols,
    tile_count,
    send_lower,
    send_upper,
    assign,
    w_coarse,
    coarse_adj,
):
    vertex_rows = features.shape[0]
    feat_width = features.shape[1]
    block_rows = adj_tiles.shape[2]
    slot_count = adj_tiles.shape[1]
    block_count = vertex_rows // block_rows
    halo_blocks = send_lower.shape[0]
    projected = jnp.dot(features, w_fine, preferred_element_type=jnp.float32).astype(jnp.bfloat16)
    own_blocks = projected.reshape(block_count, block_rows, feat_width)
    lower_sel = own_blocks[send_lower]
    upper_sel = own_blocks[send_upper]
    packed = jnp.concatenate([lower_sel, upper_sel], axis=0).reshape(
        2 * halo_blocks * block_rows, feat_width
    )
    padded = with_halo(packed, ((DOM, 0),), halo_blocks * block_rows)
    from_below = padded[: halo_blocks * block_rows].reshape(halo_blocks, block_rows, feat_width)
    from_above = padded[-halo_blocks * block_rows :].reshape(halo_blocks, block_rows, feat_width)
    extended = jnp.concatenate([own_blocks, from_below, from_above], axis=0)
    coarse_sums = jax.ops.segment_sum(features.astype(jnp.float32), assign, num_segments=NC)
    counts = jax.ops.segment_sum(jnp.ones((vertex_rows,), jnp.float32), assign, num_segments=NC)
    live_mask = jnp.arange(slot_count)[None, :] < tile_count[:, None]
    kept = jnp.where(live_mask[:, :, None, None], adj_tiles, jnp.zeros((), jnp.bfloat16))
    picked = extended[tile_cols]
    fine_out = jnp.einsum("rkij,rkjf->rif", kept, picked, preferred_element_type=jnp.float32)
    fine_out = fine_out.reshape(vertex_rows, feat_width)
    share_sums, share_counts = sent_together(
        (coarse_sums.astype(jnp.bfloat16), counts.astype(jnp.bfloat16)), DOM, 0, 1
    )
    share_sums, share_counts = (
        over_copies(share_sums.astype(jnp.bfloat16), GRP).astype(jnp.float32),
        over_copies(share_counts.astype(jnp.bfloat16), GRP).astype(jnp.float32),
    )
    coarse_all = collect(finish(share_sums, share_counts, w_coarse), DOM, 0)
    own_count = coarse_adj.shape[0]
    own_start = (lax.axis_index(DOM) * lax.axis_size(GRP) + lax.axis_index(GRP)) * own_count
    self_rows = lax.dynamic_slice_in_dim(coarse_all, own_start, own_count, 0)
    coarse_mixed = (
        self_rows.astype(jnp.float32)
        + jnp.dot(coarse_adj, coarse_all, preferred_element_type=jnp.float32)
    ).astype(jnp.bfloat16)
    coarse_every = gather_axes(coarse_mixed, DOM_GRP, (0, 2, 3, 1), 0)
    return jax.nn.relu(fine_out + coarse_every[assign].astype(jnp.float32)).astype(jnp.bfloat16)


def solution(mesh):
    finer = Mesh(mesh.devices.reshape(4, 2, 4, 4), ("dom_0", "dom_1", "grp_0", "grp_1"))
    placed = (
        P(DOM_GRP, None),
        P(),
        P(DOM_GRP, None, None, None),
        P(DOM_GRP, None),
        P(DOM_GRP),
        P(DOM_GRP),
        P(DOM_GRP),
        P(DOM_GRP),
        P(),
        P(DOM_GRP, None),
    )
    return jax.shard_map(
        per_device, mesh=finer, in_specs=placed, out_specs=P(DOM_GRP, None), check_vma=False
    )
```

profile of v0, /device:TPU:1, one launch (start us, length us, event | category | flops | bytes accessed | tf_op | source)
XLA Modules:
  0.0 200.0 jit_solution(16795491740894961772)
XLA Ops:
  0.0 29.1 %scatter_custom_fusion.1 = f32[1024]{0:T(1024)S(1)} fusion(s32[4096]{0:T(1024)} %param.17, f32[4096]{0:T(1024)S(1)} %broadcast.28, f32[]{:T(128)} %constant.20.clone.1), kind=kCustom, calls=%fused_computation.37 | custom fusion | flops 4096 | bytes 4608 | tf_op jit(solution)/shard_map/scatter-add | solution.py:123
  29.1 21.1 %scatter_custom_fusion = f32[1024,256]{1,0:T(8,128)S(1)} fusion(s32[4096]{0:T(1024)} %param.17, bf16[4096,256]{1,0:T(8,128)(2,1)} %param.10, f32[]{:T(128)} %constant.20.clone.1), kind=kCustom, calls=%fused_computation.14 | custom fusion | flops 2097152 | bytes 3146240 | tf_op jit(solution)/shard_map/scatter-add | solution.py:122
  50.3 0.3 copy.38
  50.6 0.9 pad_maximum_fusion.1
  51.4 5.8 %all-to-all-start = ((bf16[8,128,257]{1,2,0:T(8,128)(2,1)}), bf16[8,128,257]{1,2,0:T(8,128)(2,1)S(1)}, u32[]{:S(2)}, u32[]{:S(2)}) async-start(bf16[8,128,257]{1,2,0:T(8,128)(2,1)} %pad_maximum_fusion.1), calls=%async_computation | async-start | bytes 1081344 | tf_op jit(solution)/shard_map/all_to_all | solution.py:36
  57.3 2.3 %convolution_convert_fusion = bf16[4096,256]{1,0:T(8,128)(2,1)S(1)} fusion(bf16[4096,256]{1,0:T(8,128)(2,1)} %param.10, bf16[256,256]{1,0:T(8,128)(2,1)S(1)} %copy-done), kind=kOutput, calls=%fused_computation.10 | convolution fusion | flops 537919488 | bytes 4325376 | tf_op jit(solution)/shard_map/dot_general | solution.py:111
  59.6 0.6 gather_fusion.1
  60.3 6.5 %all-to-all-done = bf16[8,128,257]{1,2,0:T(8,128)(2,1)S(1)} async-done(((bf16[8,128,257]{1,2,0:T(8,128)(2,1)}), bf16[8,128,257]{1,2,0:T(8,128)(2,1)S(1)}, u32[]{:S(2)}, u32[]{:S(2)}) %all-to-all-start) | async-done | bytes 526368 | tf_op jit(solution)/shard_map/all_to_all | solution.py:36
  66.9 0.6 broadcast_in_dim.69
  67.5 7.8 %all-to-all-start.2 = ((bf16[16,1,128]{2,1,0:T(2,128)(2,1)}), bf16[16,1,128]{2,1,0:T(2,128)(2,1)S(1)}, u32[]{:S(2)}, u32[]{:S(2)}) async-start(bf16[16,1,128]{2,1,0:T(2,128)(2,1)} %broadcast_in_dim.69), calls=%async_computation.2 | async-start | bytes 16384 | tf_op jit(solution)/shard_map/all_to_all | solution.py:54
  75.2 0.6 gather_fusion
  75.8 1.5 collective-permute-start
  77.4 0.1 copy.45
  77.5 4.0 %all-to-all-done.2 = bf16[16,1,128]{2,1,0:T(2,128)(2,1)S(1)} async-done(((bf16[16,1,128]{2,1,0:T(2,128)(2,1)}), bf16[16,1,128]{2,1,0:T(2,128)(2,1)S(1)}, u32[]{:S(2)}, u32[]{:S(2)}) %all-to-all-start.2) | async-done | bytes 4128 | tf_op jit(solution)/shard_map/all_to_all | solution.py:54
  81.5 1.1 broadcast_in_dim.68
  82.6 4.3 %all-to-all-start.1 = ((bf16[16,128,256]{2,1,0:T(8,128)(2,1)}), bf16[16,128,256]{2,1,0:T(8,128)(2,1)}, u32[]{:S(2)}, u32[]{:S(2)}) async-start(bf16[16,128,256]{2,1,0:T(8,128)(2,1)} %broadcast_in_dim.68), calls=%async_computation.1 | async-start | bytes 2097152 | tf_op jit(solution)/shard_map/all_to_all | solution.py:54
  87.2 0.7 iota_compare_fusion
  87.9 0.6 fusion.12
  88.5 1.9 pad_maximum_fusion
  90.4 19.3 %gather_fusion.2 = bf16[640,128,256]{2,1,0:T(8,128)(2,1)} fusion(bf16[40,128,256]{2,1,0:T(8,128)(2,1)S(1)} %pad_maximum_fusion, s32[1024]{0:T(1024)S(1)} %pad_clamp_fusion), kind=kCustom, calls=%fused_computation.2 | custom fusion | bytes 83888640 | tf_op jit(solution)/shard_map/gather | solution.py:126
  109.8 1.4 convert_reduce_fusion
  111.2 0.2 convolution_convert_fusion.1
  111.4 0.8 broadcast_in_dim.70
  112.2 5.9 %all-to-all-start.3 = ((bf16[8,128,256]{2,1,0:T(8,128)(2,1)}), bf16[8,128,256]{2,1,0:T(8,128)(2,1)S(1)}, u32[]{:S(2)}, u32[]{:S(2)}) async-start(bf16[8,128,256]{2,1,0:T(8,128)(2,1)} %broadcast_in_dim.70), calls=%async_computation.3 | async-start | bytes 1048576 | tf_op jit(solution)/shard_map/all_to_all | solution.py:54
  118.1 23.2 %fusion = f32[32,128,256,1]{2,1,3,0:T(8,128)} fusion(bf16[32,20,128,256]{3,2,1,0:T(8,128)(2,1)} %bitcast.41, bf16[32,20,128,128]{3,2,1,0:T(8,128)(2,1)} %param.12, pred[32,20]{1,0:T(8,128)(4,1)S(1)} %copy-done.7), kind=kOutput, calls=%fused_computation.6 | convolution fusion | flops 5379194880 | bytes 67109504 | tf_op jit(solution)/shard_map/rkij,rkjf->rif/dot_general | solution.py:127
  141.4 0.2 fusion.9
  141.6 9.6 %all-gather = bf16[32,256]{1,0:T(8,128)(2,1)S(1)} all-gather(bf16[8,256]{1,0:T(8,128)(2,1)S(1)} %fusion.9), channel_id=2, replica_groups=mesh['dom_0'=4,'dom_1'=2,'grp_0'=4,'grp_1'=4] {'dom_0'}, dimensions={0}, use_global_device_ids=true | all-gather | bytes 20480 | tf_op jit(solution)/shard_map/all_gather | solution.py:77
  151.2 9.6 %all-gather.1 = bf16[16,8,256]{2,1,0:T(8,128)(2,1)S(1)} all-gather(bf16[4,8,256]{2,1,0:T(8,128)(2,1)S(1)} %bitcast.54), channel_id=3, replica_groups=mesh['dom_0'=4,'dom_1'=2,'grp_0'=4,'grp_1'=4] {'grp_0'}, dimensions={0}, use_global_device_ids=true | all-gather | bytes 81920 | tf_op jit(solution)/shard_map/all_gather | solution.py:77
  160.7 9.7 %all-gather.2 = bf16[16,4,8,256]{3,2,1,0:T(8,128)(2,1)S(1)} all-gather(bf16[4,4,8,256]{3,2,1,0:T(8,128)(2,1)S(1)} %bitcast.51), channel_id=4, replica_groups=mesh['dom_0'=4,'dom_1'=2,'grp_0'=4,'grp_1'=4] {'grp_1'}, dimensions={0}, use_global_device_ids=true | all-gather | bytes 327680 | tf_op jit(solution)/shard_map/all_gather | solution.py:77
  170.4 10.9 %all-gather.3 = bf16[8,4,4,8,256]{4,3,2,1,0:T(8,128)(2,1)S(1)} all-gather(bf16[4,4,4,8,256]{4,3,2,1,0:T(8,128)(2,1)S(1)} %bitcast.48), channel_id=5, replica_groups=mesh['dom_0'=4,'dom_1'=2,'grp_0'=4,'grp_1'=4] {'dom_1'}, dimensions={0}, use_global_device_ids=true | all-gather | bytes 786432 | tf_op jit(solution)/shard_map/all_gather | solution.py:77
  181.3 14.6 %gather_fusion.3 = bf16[4096,256]{1,0:T(8,128)(2,1)S(1)} fusion(bf16[1024,256]{1,0:T(8,128)(2,1)S(1)} %bitcast.40, s32[4096]{0:T(1024)S(1)} %copy-done.3), kind=kCustom, calls=%fused_computation.3 | custom fusion | bytes 4210688 | tf_op jit(solution)/shard_map/gather | solution.py:145
  196.0 4.0 %fusion.5 = bf16[4096,256]{1,0:T(8,128)(2,1)} fusion(f32[32,128,256,1]{2,1,3,0:T(8,128)} %fusion, bf16[4096,256]{1,0:T(8,128)(2,1)S(1)} %gather_fusion.3), kind=kLoop, calls=%fused_computation.13 | loop fusion | flops 4194304 | bytes 8388608 | tf_op jit(solution)/shard_map/convert_element_type | solution.py:145
  (47 shorter events, 0.5 us)
Async XLA Ops:
  0.0 57.3 %copy-start = (bf16[256,256]{1,0:T(8,128)(2,1)S(1)}, bf16[256,256]{1,0:T(8,128)(2,1)}, u32[]{:S(2)}) copy-start(bf16[256,256]{1,0:T(8,128)(2,1)} %param.11) | copy-start | bytes 393220
  50.2 7.0 %copy-start.10 = (s32[4]{0:T(128)S(1)}, s32[4]{0:T(128)}, u32[]{:S(2)}) copy-start(s32[4]{0:T(128)} %param.15) | copy-start | bytes 52
  51.4 15.3 %all-to-all-start = ((bf16[8,128,257]{1,2,0:T(8,128)(2,1)}), bf16[8,128,257]{1,2,0:T(8,128)(2,1)S(1)}, u32[]{:S(2)}, u32[]{:S(2)}) async-start(bf16[8,128,257]{1,2,0:T(8,128)(2,1)} %pad_maximum_fusion.1), calls=%async_computation | async-start | bytes 1081344 | tf_op jit(solution)/shard_map/all_to_all | solution.py:36
  57.3 3.0 %copy-start.11 = (s32[4]{0:T(128)S(1)}, s32[4]{0:T(128)}, u32[]{:S(2)}) copy-start(s32[4]{0:T(128)} %param.16) | copy-start | bytes 52
  59.6 27.6 %copy-start.2 = (bf16[4096,256]{1,0:T(8,128)(2,1)}, bf16[4096,256]{1,0:T(8,128)(2,1)S(1)}, u32[]{:S(2)}) copy-start(bf16[4096,256]{1,0:T(8,128)(2,1)S(1)} %convolution_convert_fusion) | copy-start | bytes 6291460
  59.6 27.4 %copy-start.6 = (s32[32,20]{0,1:T(8,128)S(1)}, s32[32,20]{0,1:T(8,128)}, u32[]{:S(2)}) copy-start(s32[32,20]{0,1:T(8,128)} %param.13) | copy-start | bytes 7684
  59.6 27.6 %copy-start.8 = (s32[32]{0:T(128)S(1)}, s32[32]{0:T(128)}, u32[]{:S(2)}) copy-start(s32[32]{0:T(128)} %param.14) | copy-start | bytes 388
  59.6 28.3 %copy-start.5 = (s32[4096]{0:T(1024)S(1)}, s32[4096]{0:T(1024)}, u32[]{:S(2)}) copy-start(s32[4096]{0:T(1024)} %param.17) | copy-start | bytes 49156
  60.2 28.3 %collective-permute-start.1 = (bf16[512,256]{1,0:T(8,128)(2,1)S(1)}, bf16[512,256]{1,0:T(8,128)(2,1)S(1)}, u32[]{:S(2)}, u32[]{:S(2)}) collective-permute-start(bf16[512,256]{1,0:T(8,128)(2,1)S(1)} %bitcast.52), channel_id=1, source_target_pairs={{16,0},{32,16},{48,32},{64,48},{80,64},{96,80},{112,96},{0,112},{1... | collective-permute-start | bytes 786440 | tf_op jit(solution)/shard_map/ppermute | solution.py:23
  67.5 14.1 %all-to-all-start.2 = ((bf16[16,1,128]{2,1,0:T(2,128)(2,1)}), bf16[16,1,128]{2,1,0:T(2,128)(2,1)S(1)}, u32[]{:S(2)}, u32[]{:S(2)}) async-start(bf16[16,1,128]{2,1,0:T(2,128)(2,1)} %broadcast_in_dim.69), calls=%async_computation.2 | async-start | bytes 16384 | tf_op jit(solution)/shard_map/all_to_all | solution.py:54
  75.8 12.7 %collective-permute-start = (bf16[512,256]{1,0:T(8,128)(2,1)S(1)}, bf16[512,256]{1,0:T(8,128)(2,1)S(1)}, u32[]{:S(2)}, u32[]{:S(2)}) collective-permute-start(bf16[512,256]{1,0:T(8,128)(2,1)S(1)} %bitcast.53), channel_id=1, source_target_pairs={{0,16},{16,32},{32,48},{48,64},{64,80},{80,96},{96,112},{112,0},{1... | collective-permute-start | bytes 786440 | tf_op jit(solution)/shard_map/ppermute | solution.py:22
  82.6 27.1 %all-to-all-start.1 = ((bf16[16,128,256]{2,1,0:T(8,128)(2,1)}), bf16[16,128,256]{2,1,0:T(8,128)(2,1)}, u32[]{:S(2)}, u32[]{:S(2)}) async-start(bf16[16,128,256]{2,1,0:T(8,128)(2,1)} %broadcast_in_dim.68), calls=%async_computation.1 | async-start | bytes 2097152 | tf_op jit(solution)/shard_map/all_to_all | solution.py:54
  90.4 20.7 %copy-start.9 = (bf16[256,256]{1,0:T(8,128)(2,1)S(1)}, bf16[256,256]{1,0:T(8,128)(2,1)}, u32[]{:S(2)}) copy-start(bf16[256,256]{1,0:T(8,128)(2,1)} %param.18) | copy-start | bytes 393220
  109.7 8.4 %copy-start.7 = (pred[32,20]{1,0:T(8,128)(4,1)S(1)}, pred[32,20]{1,0:T(8,128)(4,1)}, u32[]{:S(2)}) copy-start(pred[32,20]{1,0:T(8,128)(4,1)} %iota_compare_fusion) | copy-start | bytes 1924
  112.2 29.2 %all-to-all-start.3 = ((bf16[8,128,256]{2,1,0:T(8,128)(2,1)}), bf16[8,128,256]{2,1,0:T(8,128)(2,1)S(1)}, u32[]{:S(2)}, u32[]{:S(2)}) async-start(bf16[8,128,256]{2,1,0:T(8,128)(2,1)} %broadcast_in_dim.70), calls=%async_computation.3 | async-start | bytes 1048576 | tf_op jit(solution)/shard_map/all_to_all | solution.py:54
  118.1 23.2 %copy-start.4 = (bf16[8,1024]{1,0:T(8,128)(2,1)S(1)}, bf16[8,1024]{1,0:T(8,128)(2,1)}, u32[]{:S(2)}) copy-start(bf16[8,1024]{1,0:T(8,128)(2,1)} %param.19) | copy-start | bytes 49156
  141.4 39.9 %copy-start.3 = (s32[4096]{0:T(1024)S(1)}, s32[4096]{0:T(1024)}, u32[]{:S(2)}) copy-start(s32[4096]{0:T(1024)} %fusion.12) | copy-start | bytes 49156
  181.3 18.7 %copy-start.1 = (bf16[256,256]{1,0:T(8,128)(2,1)S(1)}, bf16[256,256]{1,0:T(8,128)(2,1)}, u32[]{:S(2)}) copy-start(bf16[256,256]{1,0:T(8,128)(2,1)} %param.11) | copy-start | bytes 393220
where the time goes:
time: 201 us; the launch traced here: 200 us
  other arithmetic  59.8 us (30%)
  blocking collectives  39.7 us (20%)
  local copies, waits for them, and re-layouts  38.3 us (19%)
  matrix products  25.9 us (13%)
  starting transfers between devices  25.4 us (13%)
  waiting for transfers between devices  10.6 us (5%)
    all_gather x4, blocking collectives, gather_in_order(): blocks = lax.all_gather(blocks, axes[k])  39.7 us
    scatter-add x1, other arithmetic, per_device(): jax.ops.segment_sum(jnp.ones((vertex_rows,), jnp.float32), assign, num_se...  29.1 us
    dot_general x1, matrix products, per_device(): jnp.einsum('rkij,rkjf->rif', kept, picked, preferred_element_type=jnp.flo...  23.2 us
    scatter-add x1, other arithmetic, per_device(): jax.ops.segment_sum(features.astype(jnp.float32), assign, num_segments=NC)  21.1 us
    gather x1, local copies, waits for them, and re-layouts, per_device(): picked = extended[tile_cols]  19.3 us
    all_to_all x3, starting transfers between devices, from_everyone(): lax.all_to_all(jnp.broadcast_to(shard[None], (peers, *shard.shape)), axis...  18 us
    gather x1, local copies, waits for them, and re-layouts, per_device(): coarse_every[assign].astype(jnp.float32)  14.6 us
    all_to_all x1, waiting for transfers between devices, sent_and_summed(): lax.all_to_all(in_blocks(shard, dim, peers), axis, 0, 0, tiled=True)  6.5 us
  transfers between devices with their start and end apart: 6, of which 2 were waited for; matrix products, arithmetic and copies ran while one was open for 26% of the time, Pallas kernels for 0%

commit v1 on v0

v1 whole, which is shorter than its diff:
```python
import jax
import jax.numpy as jnp
from jax import lax
from jax.experimental import pallas as pl
from jax.experimental.pallas import tpu as pltpu
from jax.sharding import PartitionSpec as P

MESH = pl.DeviceIdType.MESH
F = 256
BS = 128
K = 20
H = 4
NC = 1024
V = 4096
NB = 32
BF = jnp.bfloat16
F32 = jnp.float32
ADJ_CHUNK = 4
FEAT_CHUNK = 1024
OUT_CHUNK = 512


def ring_hops(d):
    return min(d % 4, -d % 4)


OFFSETS = sorted(
    [
        (ox, oz, oy)
        for ox in range(4)
        for oz in range(4)
        for oy in range(4)
        if (ox, oz, oy) != (0, 0, 0)
    ],
    key=lambda o: -sum(ring_hops(d) for d in o),
)


def wait_bytes(ref, sem):
    pltpu.make_async_copy(ref, ref, sem).wait()


def send(src, dst, ssem, rsem, to):
    pltpu.make_async_remote_copy(
        src, dst, ssem, rsem, device_id=to, device_id_type=MESH
    ).start()


def rows_of(pieces):
    wide = pieces.astype(F32)
    n = wide.shape[0]
    low = wide[:, :8, :].reshape(n * 8, 128)
    high = wide[:, 8:16, :].reshape(n * 8, 128)
    return jnp.concatenate([low, high], axis=1)


def piece_of(rows):
    return jnp.concatenate([rows[:, :128], rows[:, 128:]], axis=0).astype(BF)


def kernel(
    feat_hbm, wf_ref, adj_hbm, pick_ref, lower_ref, upper_ref, assign_ref, wc_ref,
    cadj_ref, out_hbm,
    feat, adj, ext, fine, onehot, acol, out, half, hits, core_send, core_recv, rs_send, rs_recv,
    halo, gath, own_piece, table,
    feat_sem, adj_sem, out_sem, core_sems, rs_sems, halo_sems, ag_sems,
):
    dom = lax.axis_index("dom")
    grp = lax.axis_index("grp")
    x, core = dom // 2, dom % 2
    z, y = grp // 4, grp % 4
    chip = x * 16 + grp
    place = dom * 16 + grp

    def chip_at(o):
        return (x + o[0]) % 4, ((z + o[1]) % 4) * 4 + (y + o[2]) % 4

    def same_core(o):
        to_x, to_grp = chip_at(o)
        return {"dom": to_x * 2 + core, "grp": to_grp}

    partner = {"dom": x * 2 + 1 - core, "grp": grp}
    upper = {"dom": (dom + 1) % 8, "grp": grp}
    lower = {"dom": (dom + 7) % 8, "grp": grp}
    across = {"dom": (dom + core * 2 + 7) % 8, "grp": grp}

    feat_copies = []
    for i in range(V // FEAT_CHUNK):
        part = pl.ds(i * FEAT_CHUNK // BS, FEAT_CHUNK // BS)
        c = pltpu.make_async_copy(feat_hbm.at[part], feat.at[part], feat_sem.at[i])
        c.start()
        feat_copies.append(c)
    barrier = pltpu.get_barrier_semaphore()
    for o in OFFSETS:
        pl.semaphore_signal(barrier, inc=1, device_id=same_core(o), device_id_type=MESH)
    pl.semaphore_signal(barrier, inc=1, device_id=partner, device_id_type=MESH)
    pl.semaphore_signal(barrier, inc=1, device_id=across, device_id_type=MESH)
    adj_copies = []
    for i in range(NB // ADJ_CHUNK):
        part = pl.ds(i * ADJ_CHUNK, ADJ_CHUNK)
        c = pltpu.make_async_copy(adj_hbm.at[part], adj.at[part], adj_sem.at[i])
        c.start()
        adj_copies.append(c)

    nodes = assign_ref[...]

    def segment_half(which, arrive):
        local = jnp.where(
            (nodes // 128) % 2 == which, (nodes // 256) * 128 + nodes % 128, -1
        )
        half[...] = jnp.zeros_like(half)
        hits[...] = jnp.zeros_like(hits)
        acol[0, 0:32, :] = local
        for i in range(V // FEAT_CHUNK):
            if arrive:
                feat_copies[i].wait()

            def strip(m, carry):
                base = m * 128
                seat = lax.broadcasted_iota(jnp.int32, (128, 128), 0) + base
                total = jnp.zeros((128, F), F32)
                count = jnp.zeros((128, 128), BF)
                for t in range(FEAT_CHUNK // 256):
                    pair = []
                    for s in range(2):
                        row = i * (FEAT_CHUNK // 128) + 2 * t + s
                        hit = jnp.where(acol[0, row : row + 1, :] == seat, 1.0, 0.0).astype(BF)
                        count = count + hit
                        pair.append(hit)
                    start = i * FEAT_CHUNK + t * 256
                    total = total + jnp.dot(
                        jnp.concatenate(pair, axis=1),
                        feat[pl.ds(start // BS, 2)].reshape(256, F),
                        preferred_element_type=F32,
                    )
                part = pl.ds(pl.multiple_of(base, 128), 128)
                half[part, :] += total
                hits[part, :] += count
                return carry

            lax.fori_loop(0, 4, strip, 0)
        counts = jnp.dot(hits[...], jnp.ones((128, 128), BF), preferred_element_type=F32)
        sums = half[...].reshape(64, 8, F)
        return jnp.concatenate(
            [sums[:, :, :128], sums[:, :, 128:], counts.reshape(64, 8, 128)], axis=1
        )

    core_send[...] = segment_half(1 - core, True).astype(BF)
    pl.semaphore_wait(barrier, len(OFFSETS) + 2)
    send(core_send, core_recv, core_sems.at[0], core_sems.at[1], partner)
    mine = segment_half(core, False)
    wait_bytes(core_recv, core_sems.at[1])
    rs_send[...] = (mine + core_recv[...].astype(F32)).astype(BF)
    for o in OFFSETS:
        to_x, to_grp = chip_at(o)
        send(
            rs_send.at[to_x * 16 + to_grp], rs_recv.at[chip], rs_sems.at[0], rs_sems.at[1],
            same_core(o),
        )
    rs_recv[chip] = rs_send[chip]

    for i in range(H):
        for side, ref in enumerate((lower_ref, upper_ref)):
            block = feat[ref[i]]
            halo[side, i] = jnp.dot(block, wf_ref[...], preferred_element_type=F32).astype(BF)
    send(halo.at[0], ext.at[pl.ds(NB + H, H)], halo_sems.at[0], halo_sems.at[1], lower)
    send(halo.at[1], ext.at[pl.ds(NB, H)], halo_sems.at[2], halo_sems.at[3], upper)

    def project(i, carry):
        block = feat[pl.ds(i * 4, 4)].reshape(512, F)
        rows = jnp.dot(block, wf_ref[...], preferred_element_type=F32).astype(BF)
        ext[pl.ds(i * 4, 4)] = rows.reshape(4, BS, F)
        return carry

    lax.fori_loop(0, V // 512, project, 0)
    ext[NB + 2 * H] = jnp.zeros((BS, F), BF)

    turned = nodes.astype(F32).T
    for r in range(NB):
        acol[r] = jnp.broadcast_to(turned[:, r : r + 1], (BS, 128)).astype(jnp.int32)
    lanes = lax.broadcasted_iota(jnp.int32, (BS, 128), 1)

    def spread(r, carry):
        col = acol[r]
        for j in range(NC // 128):
            hit = jnp.where(col == lanes + j * 128, 1.0, 0.0).astype(BF)
            onehot[pl.ds(pl.multiple_of(r * BS, BS), BS), j * 128 : (j + 1) * 128] = hit
        return carry

    lax.fori_loop(0, NB, spread, 0)

    def spmm(r, carry):
        total = jnp.zeros((BS, F), F32)
        for k in range(0, K, 2):
            tiles = jnp.concatenate([adj[r, k], adj[r, k + 1]], axis=1)
            blocks = jnp.concatenate([ext[pick_ref[r, k]], ext[pick_ref[r, k + 1]]], axis=0)
            total = total + jnp.dot(tiles, blocks, preferred_element_type=F32)
        fine[pl.ds(pl.multiple_of(r * BS, BS), BS), :] = total
        return carry

    def gather_all(step, piece):
        buf = gath.at[step]
        own_piece[step] = piece
        buf[place] = piece
        for o in OFFSETS:
            send(
                own_piece.at[step], buf.at[place], ag_sems.at[step, 0], ag_sems.at[step, 1],
                same_core(o),
            )

    def gather_cores(step):
        buf = gath.at[step]
        wait_bytes(buf.at[pl.ds(0, 63)], ag_sems.at[step, 1])
        for i in range(4):
            part = buf.at[pl.ds(i * 32 + core * 16, 16)]
            send(part, part, ag_sems.at[step, 2], ag_sems.at[step, 3], partner)
        wait_bytes(buf.at[pl.ds(0, 64)], ag_sems.at[step, 3])

    wait_bytes(rs_recv.at[pl.ds(0, 63)], rs_sems.at[1])
    whole = jnp.sum(rs_recv[...].astype(F32), axis=0)
    root = jnp.sqrt(whole[16:24, :])
    coarse = jnp.concatenate([whole[:8, :] / root, whole[8:16, :] / root], axis=1).astype(BF)
    projected = jnp.dot(coarse, wc_ref[...], preferred_element_type=F32)
    gather_all(0, piece_of(projected))

    wait_bytes(ext.at[pl.ds(NB, H)], halo_sems.at[1])
    wait_bytes(ext.at[pl.ds(NB, H)], halo_sems.at[3])
    for i in range(4):
        adj_copies[i].wait()
    lax.fori_loop(0, 16, spmm, 0)

    gather_cores(0)
    mixed = jnp.dot(cadj_ref[...], rows_of(gath[0]).astype(BF), preferred_element_type=F32)
    gather_all(1, piece_of(mixed + projected.astype(BF).astype(F32)))

    for i in range(4, 8):
        adj_copies[i].wait()
    lax.fori_loop(16, 32, spmm, 0)

    gather_cores(1)
    table[...] = rows_of(gath[1]).astype(BF)

    for i in range(V // OUT_CHUNK):
        part = pl.ds(i * OUT_CHUNK, OUT_CHUNK)
        got = jnp.dot(onehot[part, :], table[...], preferred_element_type=F32)
        out[part, :] = jnp.maximum(fine[part, :] + got, 0.0).astype(BF)
        pltpu.make_async_copy(out.at[part], out_hbm.at[part], out_sem.at[i]).start()

    wait_bytes(core_send, core_sems.at[0])
    wait_bytes(rs_send.at[pl.ds(0, 63)], rs_sems.at[0])
    wait_bytes(halo.at[0], halo_sems.at[0])
    wait_bytes(halo.at[1], halo_sems.at[2])
    for step in range(2):
        wait_bytes(gath.at[step, pl.ds(0, 63)], ag_sems.at[step, 0])
        wait_bytes(gath.at[step, pl.ds(0, 64)], ag_sems.at[step, 2])
    for i in range(V // OUT_CHUNK):
        part = pl.ds(i * OUT_CHUNK, OUT_CHUNK)
        pltpu.make_async_copy(out.at[part], out_hbm.at[part], out_sem.at[i]).wait()


def per_device(
    features, w_fine, adj_tiles, tile_cols, tile_count, send_lower, send_upper, assign, w_coarse,
    coarse_adj,
):
    vmem = pl.BlockSpec(memory_space=pltpu.VMEM)
    smem = pl.BlockSpec(memory_space=pltpu.SMEM)
    hbm = pl.BlockSpec(memory_space=pl.ANY)
    dma = pltpu.SemaphoreType.DMA
    pick = jnp.where(jnp.arange(K)[None, :] < tile_count[:, None], tile_cols, NB + 2 * H)
    return pl.pallas_call(
        kernel,
        out_shape=jax.ShapeDtypeStruct((V, F), BF),
        in_specs=[hbm, vmem, hbm, smem, smem, smem, vmem, vmem, vmem],
        out_specs=hbm,
        scratch_shapes=[
            pltpu.VMEM((NB, BS, F), BF),
            pltpu.VMEM((NB, K, BS, BS), BF),
            pltpu.VMEM((NB + 2 * H + 1, BS, F), BF),
            pltpu.VMEM((V, F), F32),
            pltpu.VMEM((V, NC), BF),
            pltpu.VMEM((NB, BS, 128), jnp.int32),
            pltpu.VMEM((V, F), BF),
            pltpu.VMEM((NC // 2, F), F32),
            pltpu.VMEM((NC // 2, 128), BF),
            pltpu.VMEM((64, 24, 128), BF),
            pltpu.VMEM((64, 24, 128), BF),
            pltpu.VMEM((64, 24, 128), BF),
            pltpu.VMEM((64, 24, 128), BF),
            pltpu.VMEM((2, H, BS, F), BF),
            pltpu.VMEM((2, 128, 16, 128), BF),
            pltpu.VMEM((2, 16, 128), BF),
            pltpu.VMEM((NC, F), BF),
            dma((V // FEAT_CHUNK,)),
            dma((NB // ADJ_CHUNK,)),
            dma((V // OUT_CHUNK,)),
            dma((2,)),
            dma((2,)),
            dma((4,)),
            dma((2, 4)),
        ],
        compiler_params=pltpu.CompilerParams(
            collective_id=0, has_side_effects=True, vmem_limit_bytes=62 * 1024 * 1024
        ),
    )(
        features.reshape(NB, BS, F), w_fine, adj_tiles, pick, send_lower, send_upper,
        assign.reshape(NB, BS), w_coarse, coarse_adj,
    )


def solution(mesh):
    both = ("dom", "grp")
    placed = (
        P(both, None), P(), P(both, None, None, None), P(both, None), P(both), P(both), P(both),
        P(both), P(), P(both, None),
    )
    return jax.shard_map(
        per_device, mesh=mesh, in_specs=placed, out_specs=P(both, None), check_vma=False
    )
```

time: 201 us -> 49.9 us (0.25)
  other arithmetic: 59.8 us -> 1.33 us
  Pallas kernels: 0 us -> 44.5 us
  blocking collectives: 39.7 us -> 0 us
  local copies, waits for them, and re-layouts: 38.3 us -> 3.83 us
  matrix products: 25.9 us -> 0 us
  starting transfers between devices: 25.4 us -> 0 us
  waiting for transfers between devices: 10.6 us -> 0 us
    scatter-add x2 -> x0, other arithmetic: 50.2 us -> none  [the longest x1 29.1 us: per_device(): jax.ops.segment_sum(jnp.ones((vertex_rows,), jnp.float32), assign, num_se...]
    pallas_call x0 -> x1, Pallas kernels: none -> 44.5 us  [per_device(): pl.pallas_call(kernel, out_shape=jax.ShapeDtypeStruct((V, F), BF), in_spe...]
    all_gather x4 -> x0, blocking collectives: 39.7 us -> none  [gather_in_order(): blocks = lax.all_gather(blocks, axes[k])]
    gather x4 -> x0, local copies, waits for them, and re-layouts: 35 us -> none  [the longest x1 19.3 us: per_device(): picked = extended[tile_cols]]
    dot_general x4 -> x0, matrix products: 25.9 us -> none  [the longest x1 23.2 us: per_device(): jnp.einsum('rkij,rkjf->rif', kept, picked, preferred_element_type=jnp.flo...]
    all_to_all x4 -> x0, starting transfers between devices: 23.8 us -> none  [the longest x3 18 us: from_everyone(): lax.all_to_all(jnp.broadcast_to(shard[None], (peers, *shard.shape)), axis...]
    all_to_all x4 -> x0, waiting for transfers between devices: 10.6 us -> none  [the longest x1 6.5 us: sent_and_summed(): lax.all_to_all(in_blocks(shard, dim, peers), axis, 0, 0, tiled=True)]
    convert_element_type x2 -> x0, other arithmetic: 4.1 us -> none  [the longest x1 4.04 us: per_device(): jax.nn.relu(fine_out + coarse_every[assign].astype(jnp.float32))]
  transfers between devices with their start and end apart: 6 -> 0, of which waited for: 2 -> 0; matrix products, arithmetic and copies ran while one was open for 26% -> 0% of each run, Pallas kernels for 0% -> 0%
where the time goes in v1:
time: 49.9 us; the launch traced here: 49.7 us
  Pallas kernels  44.5 us (89%)
  local copies, waits for them, and re-layouts  3.83 us (8%)
  other arithmetic  1.33 us (3%)
    pallas_call x1, Pallas kernels, per_device(): pl.pallas_call(kernel, out_shape=jax.ShapeDtypeStruct((V, F), BF), in_spe...  44.5 us
    unnamed x2, local copies, waits for them, and re-layouts  3.83 us
    select_n x1, other arithmetic, per_device(): jnp.where(jnp.arange(K)[None, :] < tile_count[:, None], tile_cols, NB + 2...  1.33 us

profile of v1, /device:TPU:1, one launch (start us, length us, event | category | flops | bytes accessed | tf_op | source)
XLA Modules:
  0.0 49.7 jit_solution(15698673223860598549)
XLA Ops:
  0.0 0.8 %copy.11 = s32[32,20]{1,0:T(8,128)S(1)} copy(s32[32,20]{0,1:T(8,128)} %param.13) | data formatting | bytes 5120 | tf_op args[3]
  0.8 1.3 %fusion.pick_ref = s32[32,20]{1,0:T(8,128)} fusion(s32[32,20]{1,0:T(8,128)S(1)} %copy.11, s32[32]{0:T(128)} %param.14), kind=kLoop, calls=%fused_computation.1 | loop fusion | flops 1280 | bytes 5248 | tf_op jit(solution)/shard_map/jit(_where)/select_n | solution.py:269
  2.1 44.5 %shard_map.100 = bf16[4096,256]{1,0:T(8,128)(2,1)} custom-call(bf16[32,128,256]{2,1,0:T(8,128)(2,1)} %bitcast.2, bf16[256,256]{1,0:T(8,128)(2,1)} %wf_ref.1, bf16[32,20,128,128]{3,2,1,0:T(8,128)(2,1)} %adj_hbm.1, s32[32,20]{1,0:T(8,128)} %fusion.pick_ref, s32[4]{0:T(128)} %lower_ref.1, s32[4]{0:T(128)} %upper_ref.1, s32[32,128]{1,0:T(8,128)} %bitcast.3, ...), custom_call_target="tpu_custom_call" | custom-call | tf_op jit(solution)/shard_map/pallas_call | solution.py:270
  46.6 3.0 %copy.13 = bf16[4096,256]{1,0:T(8,128)(2,1)} copy(bf16[4096,256]{1,0:T(8,128)(2,1)} %shard_map.100) | data formatting | bytes 4194304

commit v2 on v1

--- a/solution.py
+++ b/solution.py
@@ -18,6 +18,7 @@
 ADJ_CHUNK = 4
 FEAT_CHUNK = 1024
 OUT_CHUNK = 512
+DEAD = NB + 2 * H
 
 
 def ring_hops(d):
@@ -59,11 +60,11 @@
 
 
 def kernel(
-    feat_hbm, wf_ref, adj_hbm, pick_ref, lower_ref, upper_ref, assign_ref, wc_ref,
-    cadj_ref, out_hbm,
-    feat, adj, ext, fine, onehot, acol, out, half, hits, core_send, core_recv, rs_send, rs_recv,
+    feat_hbm, wf_ref, adj_hbm, cols_hbm, live_ref, lower_ref, upper_ref, assign_ref, wc_ref,
+    cadj_ref, out,
+    feat, adj, ext, fine, onehot, acol, low, match, match16, hit, mine, cols, core_send, core_recv, rs_send, rs_recv,
     halo, gath, own_piece, table,
-    feat_sem, adj_sem, out_sem, core_sems, rs_sems, halo_sems, ag_sems,
+    feat_sem, adj_sem, cols_sem, core_sems, rs_sems, halo_sems, ag_sems,
 ):
     dom = lax.axis_index("dom")
     grp = lax.axis_index("grp")
@@ -95,6 +96,8 @@
         pl.semaphore_signal(barrier, inc=1, device_id=same_core(o), device_id_type=MESH)
     pl.semaphore_signal(barrier, inc=1, device_id=partner, device_id_type=MESH)
     pl.semaphore_signal(barrier, inc=1, device_id=across, device_id_type=MESH)
+    cols_copy = pltpu.make_async_copy(cols_hbm, cols, cols_sem)
+    cols_copy.start()
     adj_copies = []
     for i in range(NB // ADJ_CHUNK):
         part = pl.ds(i * ADJ_CHUNK, ADJ_CHUNK)
@@ -103,54 +106,65 @@
         adj_copies.append(c)
 
     nodes = assign_ref[...]
-
-    def segment_half(which, arrive):
-        local = jnp.where(
-            (nodes // 128) % 2 == which, (nodes // 256) * 128 + nodes % 128, -1
-        )
-        half[...] = jnp.zeros_like(half)
-        hits[...] = jnp.zeros_like(hits)
-        acol[0, 0:32, :] = local
-        for i in range(V // FEAT_CHUNK):
-            if arrive:
-                feat_copies[i].wait()
-
-            def strip(m, carry):
-                base = m * 128
-                seat = lax.broadcasted_iota(jnp.int32, (128, 128), 0) + base
-                total = jnp.zeros((128, F), F32)
-                count = jnp.zeros((128, 128), BF)
-                for t in range(FEAT_CHUNK // 256):
+    low[...] = nodes & 127
+    for m in range(NC // 128):
+        match[m] = jnp.where((nodes >> 7) == m, 1.0, 0.0)
+    seat = lax.broadcasted_iota(jnp.int32, (BS, 128), 0)
+
+    def hits_of(b, carry):
+        hit[b] = jnp.where(low[pl.ds(b, 1), :] == seat, 1.0, 0.0).astype(BF)
+        for m in range(NC // 128):
+            row = match[m, pl.ds(b, 1), :]
+            match16[m, b] = jnp.broadcast_to(row, (16, 128)).astype(BF)
+        return carry
+
+    lax.fori_loop(0, NB, hits_of, 0, unroll=4)
+    for c in feat_copies:
+        c.wait()
+
+    def segment_half(which, put):
+        for g in range(2):
+            total = jnp.zeros((256, F), F32)
+            counts = [jnp.zeros((128, 128), BF) for _ in range(2)]
+            for t in range(V // 256):
+                strips = []
+                for i in range(2):
+                    m = 4 * g + 2 * i + which
                     pair = []
-                    for s in range(2):
-                        row = i * (FEAT_CHUNK // 128) + 2 * t + s
-                        hit = jnp.where(acol[0, row : row + 1, :] == seat, 1.0, 0.0).astype(BF)
-                        count = count + hit
-                        pair.append(hit)
-                    start = i * FEAT_CHUNK + t * 256
-                    total = total + jnp.dot(
-                        jnp.concatenate(pair, axis=1),
-                        feat[pl.ds(start // BS, 2)].reshape(256, F),
-                        preferred_element_type=F32,
-                    )
-                part = pl.ds(pl.multiple_of(base, 128), 128)
-                half[part, :] += total
-                hits[part, :] += count
-                return carry
-
-            lax.fori_loop(0, 4, strip, 0)
-        counts = jnp.dot(hits[...], jnp.ones((128, 128), BF), preferred_element_type=F32)
-        sums = half[...].reshape(64, 8, F)
-        return jnp.concatenate(
-            [sums[:, :, :128], sums[:, :, 128:], counts.reshape(64, 8, 128)], axis=1
-        )
-
-    core_send[...] = segment_half(1 - core, True).astype(BF)
+                    for b in (2 * t, 2 * t + 1):
+                        one = hit[b] * jnp.concatenate([match16[m, b]] * 8, axis=0)
+                        counts[i] = counts[i] + one
+                        pair.append(one)
+                    strips.append(jnp.concatenate(pair, axis=1))
+                total = total + jnp.dot(
+                    jnp.concatenate(strips, axis=0),
+                    feat[pl.ds(2 * t, 2)].reshape(256, F),
+                    preferred_element_type=F32,
+                )
+            count = jnp.dot(
+                jnp.concatenate(counts, axis=0), jnp.ones((128, 128), BF),
+                preferred_element_type=F32,
+            )
+            sums = total.reshape(32, 8, F)
+            put(
+                pl.ds(32 * g, 32),
+                jnp.concatenate(
+                    [sums[:, :, :128], sums[:, :, 128:], count.reshape(32, 8, 128)], axis=1
+                ),
+            )
+
+    def put_send(part, value):
+        core_send[part] = value.astype(BF)
+
+    def put_mine(part, value):
+        mine[part] = value
+
+    segment_half(1 - core, put_send)
     pl.semaphore_wait(barrier, len(OFFSETS) + 2)
     send(core_send, core_recv, core_sems.at[0], core_sems.at[1], partner)
-    mine = segment_half(core, False)
+    segment_half(core, put_mine)
     wait_bytes(core_recv, core_sems.at[1])
-    rs_send[...] = (mine + core_recv[...].astype(F32)).astype(BF)
+    rs_send[...] = (mine[...] + core_recv[...].astype(F32)).astype(BF)
     for o in OFFSETS:
         to_x, to_grp = chip_at(o)
         send(
@@ -172,8 +186,8 @@
         ext[pl.ds(i * 4, 4)] = rows.reshape(4, BS, F)
         return carry
 
-    lax.fori_loop(0, V // 512, project, 0)
-    ext[NB + 2 * H] = jnp.zeros((BS, F), BF)
+    lax.fori_loop(0, V // 512, project, 0, unroll=4)
+    ext[DEAD] = jnp.zeros((BS, F), BF)
 
     turned = nodes.astype(F32).T
     for r in range(NB):
@@ -181,19 +195,26 @@
     lanes = lax.broadcasted_iota(jnp.int32, (BS, 128), 1)
 
     def spread(r, carry):
-        col = acol[r]
+        apart = acol[r] - lanes
+        tile = jnp.where((apart & 127) == 0, apart >> 7, -1).astype(F32).astype(BF)
+        one, none = jnp.ones((BS, 128), BF), jnp.zeros((BS, 128), BF)
         for j in range(NC // 128):
-            hit = jnp.where(col == lanes + j * 128, 1.0, 0.0).astype(BF)
-            onehot[pl.ds(pl.multiple_of(r * BS, BS), BS), j * 128 : (j + 1) * 128] = hit
+            onehot[pl.ds(pl.multiple_of(r * BS, BS), BS), j * 128 : (j + 1) * 128] = jnp.where(
+                tile == j, one, none
+            )
         return carry
 
-    lax.fori_loop(0, NB, spread, 0)
+    lax.fori_loop(0, NB, spread, 0, unroll=2)
+
+    def pick(r, k):
+        live = jnp.minimum(jnp.maximum(live_ref[r] - k, 0), 1)
+        return DEAD + (cols[k, r] - DEAD) * live
 
     def spmm(r, carry):
         total = jnp.zeros((BS, F), F32)
         for k in range(0, K, 2):
             tiles = jnp.concatenate([adj[r, k], adj[r, k + 1]], axis=1)
-            blocks = jnp.concatenate([ext[pick_ref[r, k]], ext[pick_ref[r, k + 1]]], axis=0)
+            blocks = jnp.concatenate([ext[pick(r, k)], ext[pick(r, k + 1)]], axis=0)
             total = total + jnp.dot(tiles, blocks, preferred_element_type=F32)
         fine[pl.ds(pl.multiple_of(r * BS, BS), BS), :] = total
         return carry
@@ -227,7 +248,8 @@
     wait_bytes(ext.at[pl.ds(NB, H)], halo_sems.at[3])
     for i in range(4):
         adj_copies[i].wait()
-    lax.fori_loop(0, 16, spmm, 0)
+    cols_copy.wait()
+    lax.fori_loop(0, 16, spmm, 0, unroll=4)
 
     gather_cores(0)
     mixed = jnp.dot(cadj_ref[...], rows_of(gath[0]).astype(BF), preferred_element_type=F32)
@@ -235,7 +257,7 @@
 
     for i in range(4, 8):
         adj_copies[i].wait()
-    lax.fori_loop(16, 32, spmm, 0)
+    lax.fori_loop(16, 32, spmm, 0, unroll=4)
 
     gather_cores(1)
     table[...] = rows_of(gath[1]).astype(BF)
@@ -244,7 +266,6 @@
         part = pl.ds(i * OUT_CHUNK, OUT_CHUNK)
         got = jnp.dot(onehot[part, :], table[...], preferred_element_type=F32)
         out[part, :] = jnp.maximum(fine[part, :] + got, 0.0).astype(BF)
-        pltpu.make_async_copy(out.at[part], out_hbm.at[part], out_sem.at[i]).start()
 
     wait_bytes(core_send, core_sems.at[0])
     wait_bytes(rs_send.at[pl.ds(0, 63)], rs_sems.at[0])
@@ -253,9 +274,6 @@
     for step in range(2):
         wait_bytes(gath.at[step, pl.ds(0, 63)], ag_sems.at[step, 0])
         wait_bytes(gath.at[step, pl.ds(0, 64)], ag_sems.at[step, 2])
-    for i in range(V // OUT_CHUNK):
-        part = pl.ds(i * OUT_CHUNK, OUT_CHUNK)
-        pltpu.make_async_copy(out.at[part], out_hbm.at[part], out_sem.at[i]).wait()
 
 
 def per_device(
@@ -266,12 +284,11 @@
     smem = pl.BlockSpec(memory_space=pltpu.SMEM)
     hbm = pl.BlockSpec(memory_space=pl.ANY)
     dma = pltpu.SemaphoreType.DMA
-    pick = jnp.where(jnp.arange(K)[None, :] < tile_count[:, None], tile_cols, NB + 2 * H)
     return pl.pallas_call(
         kernel,
-        out_shape=jax.ShapeDtypeStruct((V, F), BF),
-        in_specs=[hbm, vmem, hbm, smem, smem, smem, vmem, vmem, vmem],
-        out_specs=hbm,
+        out_shape=pltpu.VMEM((V, F), BF),
+        in_specs=[hbm, vmem, hbm, hbm, smem, smem, smem, vmem, vmem, vmem],
+        out_specs=vmem,
         scratch_shapes=[
             pltpu.VMEM((NB, BS, F), BF),
             pltpu.VMEM((NB, K, BS, BS), BF),
@@ -279,9 +296,12 @@
             pltpu.VMEM((V, F), F32),
             pltpu.VMEM((V, NC), BF),
             pltpu.VMEM((NB, BS, 128), jnp.int32),
-            pltpu.VMEM((V, F), BF),
-            pltpu.VMEM((NC // 2, F), F32),
-            pltpu.VMEM((NC // 2, 128), BF),
+            pltpu.VMEM((NB, 128), jnp.int32),
+            pltpu.VMEM((8, NB, 128), F32),
+            pltpu.VMEM((8, NB, 16, 128), BF),
+            pltpu.VMEM((NB, BS, 128), BF),
+            pltpu.VMEM((64, 24, 128), F32),
+            pltpu.SMEM((K, NB), jnp.int32),
             pltpu.VMEM((64, 24, 128), BF),
             pltpu.VMEM((64, 24, 128), BF),
             pltpu.VMEM((64, 24, 128), BF),
@@ -292,17 +312,17 @@
             pltpu.VMEM((NC, F), BF),
             dma((V // FEAT_CHUNK,)),
             dma((NB // ADJ_CHUNK,)),
-            dma((V // OUT_CHUNK,)),
+            dma,
             dma((2,)),
             dma((2,)),
             dma((4,)),
             dma((2, 4)),
         ],
         compiler_params=pltpu.CompilerParams(
-            collective_id=0, has_side_effects=True, vmem_limit_bytes=62 * 1024 * 1024
+            collective_id=0, has_side_effects=True, vmem_limit_bytes=52 * 1024 * 1024
         ),
     )(
-        features.reshape(NB, BS, F), w_fine, adj_tiles, pick, send_lower, send_upper,
+        features.reshape(NB, BS, F), w_fine, adj_tiles, tile_cols.T, tile_count, send_lower, send_upper,
         assign.reshape(NB, BS), w_coarse, coarse_adj,
     )
 

time: 49.9 us -> 40 us (0.80)
  Pallas kernels: 44.5 us -> 38.5 us
  local copies, waits for them, and re-layouts: 3.83 us -> 1.32 us
  other arithmetic: 1.33 us -> 0 us
    pallas_call x1, Pallas kernels: 44.5 us -> 38.5 us  [per_device(): pl.pallas_call(kernel, out_shape=pltpu.VMEM((V, F), BF), in_specs=[hbm, v...]
    unnamed x2 -> x1, local copies, waits for them, and re-layouts: 3.83 us -> 1.32 us
    select_n x1 -> x0, other arithmetic: 1.33 us -> none  [per_device(): jnp.where(jnp.arange(K)[None, :] < tile_count[:, None], tile_cols, NB + 2...]
where the time goes in v2:
time: 40 us; the launch traced here: 39.8 us
  Pallas kernels  38.5 us (96%)
  local copies, waits for them, and re-layouts  1.32 us (3%)
    pallas_call x1, Pallas kernels, per_device(): pl.pallas_call(kernel, out_shape=pltpu.VMEM((V, F), BF), in_specs=[hbm, v...  38.5 us
    unnamed x1, local copies, waits for them, and re-layouts  1.32 us

profile of v2, /device:TPU:1, one launch (start us, length us, event | category | flops | bytes accessed | tf_op | source)
XLA Modules:
  0.0 39.8 jit_solution(14550589627631157291)
XLA Ops:
  0.0 38.5 %shard_map.100 = bf16[4096,256]{1,0:T(8,128)(2,1)S(1)} custom-call(bf16[32,128,256]{2,1,0:T(8,128)(2,1)} %bitcast.3, bf16[256,256]{1,0:T(8,128)(2,1)} %wf_ref.1, bf16[32,20,128,128]{3,2,1,0:T(8,128)(2,1)} %adj_hbm.1, s32[20,32]{1,0:T(8,128)} %bitcast.5, s32[32]{0:T(128)} %live_ref.1, s32[4]{0:T(128)} %lower_ref.1, s32[4]{0:T(128)} %upper_ref.1, ...), custom_call_target="tpu_custom_call" | custom-call | tf_op jit(solution)/shard_map/pallas_call | solution.py:287
  38.5 1.3 %copy.12 = bf16[4096,256]{1,0:T(8,128)(2,1)} copy(bf16[4096,256]{1,0:T(8,128)(2,1)S(1)} %shard_map.100) | data formatting | bytes 4194304

commit v3 on v2

--- a/solution.py
+++ b/solution.py
@@ -18,6 +18,9 @@
 ADJ_CHUNK = 4
 FEAT_CHUNK = 1024
 OUT_CHUNK = 512
+STRIPS = (
+    (0, 384, ("y", "z", "x")), (384, 384, ("z", "x", "y")), (768, 256, ("x", "y", "z")),
+)
 DEAD = NB + 2 * H
 
 
@@ -63,8 +66,8 @@
     feat_hbm, wf_ref, adj_hbm, cols_hbm, live_ref, lower_ref, upper_ref, assign_ref, wc_ref,
     cadj_ref, out,
     feat, adj, ext, fine, onehot, acol, low, match, match16, hit, mine, cols, core_send, core_recv, rs_send, rs_recv,
-    halo, gath, own_piece, table,
-    feat_sem, adj_sem, cols_sem, core_sems, rs_sems, halo_sems, ag_sems,
+    halo, gath, own_piece, table, whole_adj,
+    feat_sem, adj_sem, cols_sem, core_sems, rs_sems, halo_sems, ag_sems, strip_sems, swap_sems,
 ):
     dom = lax.axis_index("dom")
     grp = lax.axis_index("grp")
@@ -104,6 +107,49 @@
         c = pltpu.make_async_copy(adj_hbm.at[part], adj.at[part], adj_sem.at[i])
         c.start()
         adj_copies.append(c)
+
+    whole_adj[x, core, z, y] = cadj_ref[...]
+    spot = {"x": x, "z": z, "y": y}
+
+    def region(free, strip, most=None):
+        at = [pl.ds(0, 4) if a in free else spot[a] for a in ("x", "z", "y")]
+        return whole_adj.at[at[0], core, at[1], at[2], :, pl.ds(strip[0], strip[1])]
+
+    def strips_go(stage):
+        for i, strip in enumerate(STRIPS):
+            free, axis = strip[2][:stage], strip[2][stage]
+            part = region(free, strip)
+            for step in (2, 1, 3):
+                o = [step if a == axis else 0 for a in ("x", "z", "y")]
+                send(part, part, strip_sems.at[i, stage, 0], strip_sems.at[i, stage, 1], same_core(o))
+
+    def strips_wait(stage, way):
+        for i, strip in enumerate(STRIPS):
+            cut = pl.ds(strip[0], strip[1])
+            if stage == 0:
+                three = whole_adj.at[0, 0, 0, pl.ds(0, 3), :, cut]
+            elif stage == 1:
+                three = whole_adj.at[0, 0, pl.ds(0, 3), pl.ds(0, 4), :, cut]
+            else:
+                three = whole_adj.at[pl.ds(0, 3), 0, pl.ds(0, 4), pl.ds(0, 4), :, cut]
+            wait_bytes(three, strip_sems.at[i, stage, way])
+
+    def halo_parts(part):
+        first = part * (H // 2)
+        for side, base in ((0, NB + H), (1, NB)):
+            yield side, pl.ds(first, H // 2), pl.ds(base + first, H // 2)
+
+    def halo_go(part):
+        for side, src, dst in halo_parts(part):
+            send(
+                halo.at[side, src], ext.at[dst], halo_sems.at[part, side, 0],
+                halo_sems.at[part, side, 1], (lower, upper)[side],
+            )
+
+    def halo_wait(way):
+        for part in range(2):
+            for side, src, dst in halo_parts(part):
+                wait_bytes(ext.at[dst], halo_sems.at[part, side, way])
 
     nodes = assign_ref[...]
     low[...] = nodes & 127
@@ -160,8 +206,14 @@
         mine[part] = value
 
     segment_half(1 - core, put_send)
+    for i in range(H):
+        for side, ref in enumerate((lower_ref, upper_ref)):
+            block = feat[ref[i]]
+            halo[side, i] = jnp.dot(block, wf_ref[...], preferred_element_type=F32).astype(BF)
     pl.semaphore_wait(barrier, len(OFFSETS) + 2)
+    strips_go(0)
     send(core_send, core_recv, core_sems.at[0], core_sems.at[1], partner)
+    halo_go(0)
     segment_half(core, put_mine)
     wait_bytes(core_recv, core_sems.at[1])
     rs_send[...] = (mine[...] + core_recv[...].astype(F32)).astype(BF)
@@ -173,13 +225,6 @@
         )
     rs_recv[chip] = rs_send[chip]
 
-    for i in range(H):
-        for side, ref in enumerate((lower_ref, upper_ref)):
-            block = feat[ref[i]]
-            halo[side, i] = jnp.dot(block, wf_ref[...], preferred_element_type=F32).astype(BF)
-    send(halo.at[0], ext.at[pl.ds(NB + H, H)], halo_sems.at[0], halo_sems.at[1], lower)
-    send(halo.at[1], ext.at[pl.ds(NB, H)], halo_sems.at[2], halo_sems.at[3], upper)
-
     def project(i, carry):
         block = feat[pl.ds(i * 4, 4)].reshape(512, F)
         rows = jnp.dot(block, wf_ref[...], preferred_element_type=F32).astype(BF)
@@ -189,6 +234,9 @@
     lax.fori_loop(0, V // 512, project, 0, unroll=4)
     ext[DEAD] = jnp.zeros((BS, F), BF)
 
+    strips_wait(0, 1)
+    strips_go(1)
+    halo_go(1)
     turned = nodes.astype(F32).T
     for r in range(NB):
         acol[r] = jnp.broadcast_to(turned[:, r : r + 1], (BS, 128)).astype(jnp.int32)
@@ -199,7 +247,8 @@
         tile = jnp.where((apart & 127) == 0, apart >> 7, -1).astype(F32).astype(BF)
         one, none = jnp.ones((BS, 128), BF), jnp.zeros((BS, 128), BF)
         for j in range(NC // 128):
-            onehot[pl.ds(pl.multiple_of(r * BS, BS), BS), j * 128 : (j + 1) * 128] = jnp.where(
+            lanes_of = pl.ds(j // 2 * 128, 128)
+            onehot[j % 2, pl.ds(pl.multiple_of(r * BS, BS), BS), lanes_of] = jnp.where(
                 tile == j, one, none
             )
         return carry
@@ -219,61 +268,57 @@
         fine[pl.ds(pl.multiple_of(r * BS, BS), BS), :] = total
         return carry
 
-    def gather_all(step, piece):
-        buf = gath.at[step]
-        own_piece[step] = piece
-        buf[place] = piece
-        for o in OFFSETS:
-            send(
-                own_piece.at[step], buf.at[place], ag_sems.at[step, 0], ag_sems.at[step, 1],
-                same_core(o),
-            )
-
-    def gather_cores(step):
-        buf = gath.at[step]
-        wait_bytes(buf.at[pl.ds(0, 63)], ag_sems.at[step, 1])
-        for i in range(4):
-            part = buf.at[pl.ds(i * 32 + core * 16, 16)]
-            send(part, part, ag_sems.at[step, 2], ag_sems.at[step, 3], partner)
-        wait_bytes(buf.at[pl.ds(0, 64)], ag_sems.at[step, 3])
-
     wait_bytes(rs_recv.at[pl.ds(0, 63)], rs_sems.at[1])
     whole = jnp.sum(rs_recv[...].astype(F32), axis=0)
     root = jnp.sqrt(whole[16:24, :])
     coarse = jnp.concatenate([whole[:8, :] / root, whole[8:16, :] / root], axis=1).astype(BF)
     projected = jnp.dot(coarse, wc_ref[...], preferred_element_type=F32)
-    gather_all(0, piece_of(projected))
-
-    wait_bytes(ext.at[pl.ds(NB, H)], halo_sems.at[1])
-    wait_bytes(ext.at[pl.ds(NB, H)], halo_sems.at[3])
+    own_piece[...] = piece_of(projected)
+    gath[place] = own_piece[...]
+    for o in OFFSETS:
+        send(own_piece, gath.at[place], ag_sems.at[0], ag_sems.at[1], same_core(o))
+    strips_wait(1, 1)
+    strips_go(2)
+    halo_wait(1)
     for i in range(4):
         adj_copies[i].wait()
     cols_copy.wait()
     lax.fori_loop(0, 16, spmm, 0, unroll=4)
 
-    gather_cores(0)
-    mixed = jnp.dot(cadj_ref[...], rows_of(gath[0]).astype(BF), preferred_element_type=F32)
-    gather_all(1, piece_of(mixed + projected.astype(BF).astype(F32)))
-
     for i in range(4, 8):
         adj_copies[i].wait()
     lax.fori_loop(16, 32, spmm, 0, unroll=4)
-
-    gather_cores(1)
-    table[...] = rows_of(gath[1]).astype(BF)
+    strips_wait(2, 1)
+    wait_bytes(gath.at[pl.ds(0, 63)], ag_sems.at[1])
+    for i in range(4):
+        part = gath.at[pl.ds(i * 32 + core * 16, 16)]
+        send(part, part, ag_sems.at[2], ag_sems.at[3], partner)
+    wait_bytes(gath.at[pl.ds(0, 64)], ag_sems.at[3])
+    coarse_all = rows_of(gath[...]).astype(BF)
+    for i in range(4):
+        lines = whole_adj[i, core].reshape(128, NC)
+        kept = rows_of(gath[pl.ds(i * 32 + core * 16, 16)])
+        mixed = jnp.dot(lines, coarse_all, preferred_element_type=F32) + kept
+        table[core, i * 128 : (i + 1) * 128, :] = mixed.astype(BF)
+    send(table.at[core], table.at[core], swap_sems.at[0], swap_sems.at[1], partner)
 
     for i in range(V // OUT_CHUNK):
         part = pl.ds(i * OUT_CHUNK, OUT_CHUNK)
-        got = jnp.dot(onehot[part, :], table[...], preferred_element_type=F32)
+        fine[part, :] += jnp.dot(onehot[core, part, :], table[core], preferred_element_type=F32)
+    wait_bytes(table.at[0], swap_sems.at[1])
+    for i in range(V // OUT_CHUNK):
+        part = pl.ds(i * OUT_CHUNK, OUT_CHUNK)
+        got = jnp.dot(onehot[1 - core, part, :], table[1 - core], preferred_element_type=F32)
         out[part, :] = jnp.maximum(fine[part, :] + got, 0.0).astype(BF)
 
     wait_bytes(core_send, core_sems.at[0])
     wait_bytes(rs_send.at[pl.ds(0, 63)], rs_sems.at[0])
-    wait_bytes(halo.at[0], halo_sems.at[0])
-    wait_bytes(halo.at[1], halo_sems.at[2])
-    for step in range(2):
-        wait_bytes(gath.at[step, pl.ds(0, 63)], ag_sems.at[step, 0])
-        wait_bytes(gath.at[step, pl.ds(0, 64)], ag_sems.at[step, 2])
+    halo_wait(0)
+    wait_bytes(gath.at[pl.ds(0, 63)], ag_sems.at[0])
+    wait_bytes(gath.at[pl.ds(0, 64)], ag_sems.at[2])
+    for stage in range(3):
+        strips_wait(stage, 0)
+    wait_bytes(table.at[0], swap_sems.at[0])
 
 
 def per_device(
@@ -294,7 +339,7 @@
             pltpu.VMEM((NB, K, BS, BS), BF),
             pltpu.VMEM((NB + 2 * H + 1, BS, F), BF),
             pltpu.VMEM((V, F), F32),
-            pltpu.VMEM((V, NC), BF),
+            pltpu.VMEM((2, V, NC // 2), BF),
             pltpu.VMEM((NB, BS, 128), jnp.int32),
             pltpu.VMEM((NB, 128), jnp.int32),
             pltpu.VMEM((8, NB, 128), F32),
@@ -307,16 +352,19 @@
             pltpu.VMEM((64, 24, 128), BF),
             pltpu.VMEM((64, 24, 128), BF),
             pltpu.VMEM((2, H, BS, F), BF),
-            pltpu.VMEM((2, 128, 16, 128), BF),
-            pltpu.VMEM((2, 16, 128), BF),
-            pltpu.VMEM((NC, F), BF),
+            pltpu.VMEM((128, 16, 128), BF),
+            pltpu.VMEM((16, 128), BF),
+            pltpu.VMEM((2, NC // 2, F), BF),
+            pltpu.VMEM((4, 2, 4, 4, 8, NC), BF),
             dma((V // FEAT_CHUNK,)),
             dma((NB // ADJ_CHUNK,)),
             dma,
             dma((2,)),
             dma((2,)),
+            dma((2, 2, 2)),
             dma((4,)),
-            dma((2, 4)),
+            dma((3, 3, 2)),
+            dma((2,)),
         ],
         compiler_params=pltpu.CompilerParams(
             collective_id=0, has_side_effects=True, vmem_limit_bytes=52 * 1024 * 1024

time: 40 us -> 36.2 us (0.905)
  Pallas kernels: 38.5 us -> 34.4 us
    pallas_call x1, Pallas kernels: 38.5 us -> 34.4 us  [per_device(): pl.pallas_call(kernel, out_shape=pltpu.VMEM((V, F), BF), in_specs=[hbm, v...]
where the time goes in v3:
time: 36.2 us; the launch traced here: 35.8 us
  Pallas kernels  34.4 us (95%)
  local copies, waits for them, and re-layouts  1.32 us (4%)
    pallas_call x1, Pallas kernels, per_device(): pl.pallas_call(kernel, out_shape=pltpu.VMEM((V, F), BF), in_specs=[hbm, v...  34.4 us
    unnamed x1, local copies, waits for them, and re-layouts  1.32 us

profile of v3, /device:TPU:1, one launch (start us, length us, event | category | flops | bytes accessed | tf_op | source)
XLA Modules:
  0.0 35.8 jit_solution(9713190388872598025)
XLA Ops:
  0.0 34.4 %shard_map.100 = bf16[4096,256]{1,0:T(8,128)(2,1)S(1)} custom-call(bf16[32,128,256]{2,1,0:T(8,128)(2,1)} %bitcast.3, bf16[256,256]{1,0:T(8,128)(2,1)} %wf_ref.1, bf16[32,20,128,128]{3,2,1,0:T(8,128)(2,1)} %adj_hbm.1, s32[20,32]{1,0:T(8,128)} %bitcast.5, s32[32]{0:T(128)} %live_ref.1, s32[4]{0:T(128)} %lower_ref.1, s32[4]{0:T(128)} %upper_ref.1, ...), custom_call_target="tpu_custom_call" | custom-call | tf_op jit(solution)/shard_map/pallas_call | solution.py:332
  34.5 1.3 %copy.12 = bf16[4096,256]{1,0:T(8,128)(2,1)} copy(bf16[4096,256]{1,0:T(8,128)(2,1)S(1)} %shard_map.100) | data formatting | bytes 4194304

commit v4 on v3

--- a/solution.py
+++ b/solution.py
@@ -19,7 +19,7 @@
 FEAT_CHUNK = 1024
 OUT_CHUNK = 512
 STRIPS = (
-    (0, 384, ("y", "z", "x")), (384, 384, ("z", "x", "y")), (768, 256, ("x", "y", "z")),
+    (0, 384, ("x", "y", "z")), (384, 384, ("x", "z", "y")), (768, 256, ("z", "y", "x")),
 )
 DEAD = NB + 2 * H
 
@@ -253,7 +253,7 @@
             )
         return carry
 
-    lax.fori_loop(0, NB, spread, 0, unroll=2)
+    lax.fori_loop(0, NB, spread, 0, unroll=4)
 
     def pick(r, k):
         live = jnp.minimum(jnp.maximum(live_ref[r] - k, 0), 1)
@@ -276,23 +276,23 @@
     own_piece[...] = piece_of(projected)
     gath[place] = own_piece[...]
     for o in OFFSETS:
-        send(own_piece, gath.at[place], ag_sems.at[0], ag_sems.at[1], same_core(o))
+        send(own_piece, gath.at[place], ag_sems.at[0], ag_sems.at[4 + o[0]], same_core(o))
     strips_wait(1, 1)
     strips_go(2)
     halo_wait(1)
     for i in range(4):
         adj_copies[i].wait()
     cols_copy.wait()
-    lax.fori_loop(0, 16, spmm, 0, unroll=4)
+    lax.fori_loop(0, 16, spmm, 0, unroll=8)
 
     for i in range(4, 8):
         adj_copies[i].wait()
-    lax.fori_loop(16, 32, spmm, 0, unroll=4)
+    lax.fori_loop(16, 32, spmm, 0, unroll=8)
+    for ox in (0, 1, 3, 2):
+        wait_bytes(gath.at[pl.ds(0, 16 if ox else 15)], ag_sems.at[4 + ox])
+        part = gath.at[pl.ds((x + 4 - ox) % 4 * 32 + core * 16, 16)]
+        send(part, part, ag_sems.at[2], ag_sems.at[3], partner)
     strips_wait(2, 1)
-    wait_bytes(gath.at[pl.ds(0, 63)], ag_sems.at[1])
-    for i in range(4):
-        part = gath.at[pl.ds(i * 32 + core * 16, 16)]
-        send(part, part, ag_sems.at[2], ag_sems.at[3], partner)
     wait_bytes(gath.at[pl.ds(0, 64)], ag_sems.at[3])
     coarse_all = rows_of(gath[...]).astype(BF)
     for i in range(4):
@@ -362,7 +362,7 @@
             dma((2,)),
             dma((2,)),
             dma((2, 2, 2)),
-            dma((4,)),
+            dma((8,)),
             dma((3, 3, 2)),
             dma((2,)),
         ],

time: 36.2 us -> 35.5 us (0.981)
  Pallas kernels: 34.4 us -> 34 us
    pallas_call x1, Pallas kernels: 34.4 us -> 34 us  [per_device(): pl.pallas_call(kernel, out_shape=pltpu.VMEM((V, F), BF), in_specs=[hbm, v...]
where the time goes in v4:
time: 35.5 us; the launch traced here: 35.4 us
  Pallas kernels  34 us (96%)
  local copies, waits for them, and re-layouts  1.32 us (4%)
    pallas_call x1, Pallas kernels, per_device(): pl.pallas_call(kernel, out_shape=pltpu.VMEM((V, F), BF), in_specs=[hbm, v...  34 us
    unnamed x1, local copies, waits for them, and re-layouts  1.32 us

profile of v4, /device:TPU:1, one launch (start us, length us, event | category | flops | bytes accessed | tf_op | source)
XLA Modules:
  0.0 35.4 jit_solution(11630557264313944138)
XLA Ops:
  0.0 34.0 %shard_map.100 = bf16[4096,256]{1,0:T(8,128)(2,1)S(1)} custom-call(bf16[32,128,256]{2,1,0:T(8,128)(2,1)} %bitcast.3, bf16[256,256]{1,0:T(8,128)(2,1)} %wf_ref.1, bf16[32,20,128,128]{3,2,1,0:T(8,128)(2,1)} %adj_hbm.1, s32[20,32]{1,0:T(8,128)} %bitcast.5, s32[32]{0:T(128)} %live_ref.1, s32[4]{0:T(128)} %lower_ref.1, s32[4]{0:T(128)} %upper_ref.1, ...), custom_call_target="tpu_custom_call" | custom-call | tf_op jit(solution)/shard_map/pallas_call | solution.py:332
  34.0 1.3 %copy.12 = bf16[4096,256]{1,0:T(8,128)(2,1)} copy(bf16[4096,256]{1,0:T(8,128)(2,1)S(1)} %shard_map.100) | data formatting | bytes 4194304

commit v5 on v4

--- a/solution.py
+++ b/solution.py
@@ -19,7 +19,7 @@
 FEAT_CHUNK = 1024
 OUT_CHUNK = 512
 STRIPS = (
-    (0, 384, ("x", "y", "z")), (384, 384, ("x", "z", "y")), (768, 256, ("z", "y", "x")),
+    (0, 256, ("z", "y", "x")), (256, 384, ("x", "y", "z")), (640, 384, ("x", "z", "y")),
 )
 DEAD = NB + 2 * H
 
@@ -66,7 +66,7 @@
     feat_hbm, wf_ref, adj_hbm, cols_hbm, live_ref, lower_ref, upper_ref, assign_ref, wc_ref,
     cadj_ref, out,
     feat, adj, ext, fine, onehot, acol, low, match, match16, hit, mine, cols, core_send, core_recv, rs_send, rs_recv,
-    halo, gath, own_piece, table, whole_adj,
+    halo, gath, own_piece, table, whole_adj, coarse, sums,
     feat_sem, adj_sem, cols_sem, core_sems, rs_sems, halo_sems, ag_sems, strip_sems, swap_sems,
 ):
     dom = lax.axis_index("dom")
@@ -123,16 +123,19 @@
                 o = [step if a == axis else 0 for a in ("x", "z", "y")]
                 send(part, part, strip_sems.at[i, stage, 0], strip_sems.at[i, stage, 1], same_core(o))
 
+    def strip_wait(i, stage, way):
+        cut = pl.ds(STRIPS[i][0], STRIPS[i][1])
+        if stage == 0:
+            three = whole_adj.at[0, 0, 0, pl.ds(0, 3), :, cut]
+        elif stage == 1:
+            three = whole_adj.at[0, 0, pl.ds(0, 3), pl.ds(0, 4), :, cut]
+        else:
+            three = whole_adj.at[pl.ds(0, 3), 0, pl.ds(0, 4), pl.ds(0, 4), :, cut]
+        wait_bytes(three, strip_sems.at[i, stage, way])
+
     def strips_wait(stage, way):
-        for i, strip in enumerate(STRIPS):
-            cut = pl.ds(strip[0], strip[1])
-            if stage == 0:
-                three = whole_adj.at[0, 0, 0, pl.ds(0, 3), :, cut]
-            elif stage == 1:
-                three = whole_adj.at[0, 0, pl.ds(0, 3), pl.ds(0, 4), :, cut]
-            else:
-                three = whole_adj.at[pl.ds(0, 3), 0, pl.ds(0, 4), pl.ds(0, 4), :, cut]
-            wait_bytes(three, strip_sems.at[i, stage, way])
+        for i in range(len(STRIPS)):
+            strip_wait(i, stage, way)
 
     def halo_parts(part):
         first = part * (H // 2)
@@ -271,8 +274,8 @@
     wait_bytes(rs_recv.at[pl.ds(0, 63)], rs_sems.at[1])
     whole = jnp.sum(rs_recv[...].astype(F32), axis=0)
     root = jnp.sqrt(whole[16:24, :])
-    coarse = jnp.concatenate([whole[:8, :] / root, whole[8:16, :] / root], axis=1).astype(BF)
-    projected = jnp.dot(coarse, wc_ref[...], preferred_element_type=F32)
+    scaled = jnp.concatenate([whole[:8, :] / root, whole[8:16, :] / root], axis=1).astype(BF)
+    projected = jnp.dot(scaled, wc_ref[...], preferred_element_type=F32)
     own_piece[...] = piece_of(projected)
     gath[place] = own_piece[...]
     for o in OFFSETS:
@@ -292,14 +295,21 @@
         wait_bytes(gath.at[pl.ds(0, 16 if ox else 15)], ag_sems.at[4 + ox])
         part = gath.at[pl.ds((x + 4 - ox) % 4 * 32 + core * 16, 16)]
         send(part, part, ag_sems.at[2], ag_sems.at[3], partner)
-    strips_wait(2, 1)
     wait_bytes(gath.at[pl.ds(0, 64)], ag_sems.at[3])
-    coarse_all = rows_of(gath[...]).astype(BF)
+    coarse[...] = rows_of(gath[...]).astype(BF)
     for i in range(4):
-        lines = whole_adj[i, core].reshape(128, NC)
-        kept = rows_of(gath[pl.ds(i * 32 + core * 16, 16)])
-        mixed = jnp.dot(lines, coarse_all, preferred_element_type=F32) + kept
-        table[core, i * 128 : (i + 1) * 128, :] = mixed.astype(BF)
+        sums[i] = rows_of(gath[pl.ds(i * 32 + core * 16, 16)])
+    for n, (start, width, _) in enumerate(STRIPS):
+        strip_wait(n, 2, 1)
+        for i in range(4):
+            lines = whole_adj[i, core, :, :, :, start : start + width].reshape(128, width)
+            total = sums[i] + jnp.dot(
+                lines, coarse[start : start + width, :], preferred_element_type=F32
+            )
+            if n < 2:
+                sums[i] = total
+            else:
+                table[core, i * 128 : (i + 1) * 128, :] = total.astype(BF)
     send(table.at[core], table.at[core], swap_sems.at[0], swap_sems.at[1], partner)
 
     for i in range(V // OUT_CHUNK):
@@ -356,6 +366,8 @@
             pltpu.VMEM((16, 128), BF),
             pltpu.VMEM((2, NC // 2, F), BF),
             pltpu.VMEM((4, 2, 4, 4, 8, NC), BF),
+            pltpu.VMEM((NC, F), BF),
+            pltpu.VMEM((4, 128, F), F32),
             dma((V // FEAT_CHUNK,)),
             dma((NB // ADJ_CHUNK,)),
             dma,

time: 35.5 us -> 35.6 us (level)
  no operation moved by 1% of the time
where the time goes in v5:
time: 35.6 us; the launch traced here: 35.4 us
  Pallas kernels  34.1 us (96%)
  local copies, waits for them, and re-layouts  1.32 us (4%)
    pallas_call x1, Pallas kernels, per_device(): pl.pallas_call(kernel, out_shape=pltpu.VMEM((V, F), BF), in_specs=[hbm, v...  34.1 us
    unnamed x1, local copies, waits for them, and re-layouts  1.32 us

profile of v5, /device:TPU:1, one launch (start us, length us, event | category | flops | bytes accessed | tf_op | source)
XLA Modules:
  0.0 35.4 jit_solution(3365409358828622231)
XLA Ops:
  0.0 34.1 %shard_map.100 = bf16[4096,256]{1,0:T(8,128)(2,1)S(1)} custom-call(bf16[32,128,256]{2,1,0:T(8,128)(2,1)} %bitcast.3, bf16[256,256]{1,0:T(8,128)(2,1)} %wf_ref.1, bf16[32,20,128,128]{3,2,1,0:T(8,128)(2,1)} %adj_hbm.1, s32[20,32]{1,0:T(8,128)} %bitcast.5, s32[32]{0:T(128)} %live_ref.1, s32[4]{0:T(128)} %lower_ref.1, s32[4]{0:T(128)} %upper_ref.1, ...), custom_call_target="tpu_custom_call" | custom-call | tf_op jit(solution)/shard_map/pallas_call | solution.py:342
  34.1 1.3 %copy.12 = bf16[4096,256]{1,0:T(8,128)(2,1)} copy(bf16[4096,256]{1,0:T(8,128)(2,1)S(1)} %shard_map.100) | data formatting | bytes 4194304
